TPU v7x, 256 devices: a whole 4x4x8 slice. The times are simulated.
256 devices in a mesh: seg: 64 (over z, x, core), mp: 4 (over y).
Axes of the slice: x: 4, y: 4, z: 8, core: 2. Of those that a mesh axis runs over, the one named last changes fastest.
Arguments:
- embedded: bfloat16 [32768, 1024], P('seg'), may hold values from -6 to 6
- targets: int32 [32768], P('seg'), may hold values from 0 to 10239
- pred_device: int32 [64], P('seg'), may hold values from -1 to 63, as said below
- doc_ids: int32 [64], P('seg'), may hold values from 0 to 15, as said below
- valid_rows: int32 [64], P('seg'), may hold values from 1 to 512, as said below
- w_query: bfloat16 [1024, 1024], P(None, 'mp'), may hold values from -8 to 8
- w_key: bfloat16 [1024, 1024], P(None, 'mp'), may hold values from -1 to 1
- w_value: bfloat16 [1024, 1024], P(None, 'mp'), may hold values from -0.1875 to 0.1875
- w_rel: bfloat16 [1024, 1024], P(None, 'mp'), may hold values from -0.1875 to 0.1875
- content_bias: float32 [16, 64], P('mp'), may hold values from -3 to 3
- position_bias: float32 [16, 64], P('mp'), may hold values from -8 to 8
- attn_out: bfloat16 [1024, 1024], P('mp'), may hold values from -0.1875 to 0.1875
- attn_gain: float32 [1024], replicated, may hold values from 0.25 to 1.75
- attn_shift: float32 [1024], replicated, may hold values from -3 to 3
- w_up: bfloat16 [1024, 4096], P(None, 'mp'), may hold values from -0.1875 to 0.1875
- up_bias: float32 [4096], P('mp'), may hold values from -3 to 3
- w_down: bfloat16 [4096, 1024], P('mp'), may hold values from -0.09375 to 0.09375
- down_bias: float32 [1024], replicated, may hold values from -3 to 3
- ffn_gain: float32 [1024], replicated, may hold values from 0.25 to 1.75
- ffn_shift: float32 [1024], replicated, may hold values from -3 to 3
- w_vocab: bfloat16 [1024, 10240], P(None, 'mp'), may hold values from -8 to 8
Outputs:
- token_loglik: float32 [32768], P('seg')
- doc_loglik: float32 [16], replicated
Inputs may be any that keep to these rules, and one draw needn't show every extreme that they name: `pred_device`: -1 for the first segment of a document, else the device of the document's previous segment, which lies from 3 devices below to 1 devices above; no device is named by two devices. `doc_ids`: every document holds one or more whole segments, chained by pred_device. `valid_rows`: 512 except on the last segment of a document.
All inputs are finite; a program needn't handle non-finite values.
Results may differ from a plain program's by a relative error of at most 0.007.
Values may be sent and summed in bfloat16 or wider, within the bound.
A program may use at most 128 MiB of HBM per device.

v0:
```python
import functools

import jax
import jax.numpy as jnp
import numpy as np
from jax import lax
from jax.experimental import pallas as pl
from jax.experimental.pallas import tpu as pltpu
from jax.sharding import PartitionSpec as P

EPSILON = 1e-05
MESH = pl.DeviceIdType.MESH
F32, BF16 = jnp.float32, jnp.bfloat16
N_X = 4
N_MP = 4
HEADS = 4
ROWS = 512
WIDTH = 1024
BLOCK = 128
HALF = 256
PIECE = 64
FINE = 32
MASKED = -1e30


def normalize(values, gain, shift):
    centre = values - jnp.mean(values, axis=-1, keepdims=True)
    spread = jnp.mean(centre * centre, axis=-1, keepdims=True)
    return centre * lax.rsqrt(spread + EPSILON) * gain + shift


def dot(a, b):
    return jnp.dot(a, b, preferred_element_type=F32)


def dot_t(a, b):
    return lax.dot_general(a, b, (((1,), (1,)), ((), ())), preferred_element_type=F32)


def kernel(
    n_seg,
    pred_s,
    doc_s,
    valid_s,
    content_bias,
    position_bias,
    basis,
    targets,
    attn_gain,
    attn_shift,
    up_bias,
    down_bias,
    ffn_gain,
    ffn_shift,
    embedded_h,
    wq_h,
    wk_h,
    wv_h,
    wr_h,
    attn_out_h,
    wup_h,
    wdown_h,
    wvocab_h,
    token_o,
    doc_o,
    emb,
    wq,
    wk,
    wv,
    wr,
    attn_out,
    wup,
    wdown,
    wvocab,
    table,
    rel,
    qc,
    qp,
    kv_own,
    kv_same,
    kv_partner,
    kv_cross,
    kv_x,
    kv_past,
    pos_past,
    top_own,
    sum_own,
    out_own,
    att_acc,
    attended,
    first_out,
    units,
    rs_send,
    rs_recv,
    second,
    stats_col,
    stats,
    doc_a,
    doc_b,
    load_sem,
    same_s,
    same_r,
    partner_s,
    partner_r,
    cross_s,
    cross_r,
    x_s,
    x_r,
    ao_s,
    ao_r,
    aof_s,
    aof_r,
    att_s,
    att_r,
    rs_s,
    rs_r,
    ag_s,
    ag_r,
    st_s,
    st_r,
    da_s,
    da_r,
    db_s,
    db_r,
):
    seg = lax.axis_index("seg")
    mp = lax.axis_index("mp")
    core = lax.rem(seg, 2)
    chip = lax.div(seg, 2)
    n_chip = n_seg // 2
    group = 2 * N_X
    n_z = n_seg // group
    in_group = lax.rem(seg, group)
    z = lax.div(seg, group)

    def chip_at(step, c):
        return (lax.rem(chip + step + n_chip, n_chip) * 2 + c, mp)

    partner = (chip * 2 + 1 - core, mp)
    forward = chip_at(1, core)
    backward = chip_at(-1, core)

    def mp_at(k):
        return (seg, lax.rem(mp + k, N_MP))

    def group_at(k):
        return (z * group + lax.rem(in_group + k, group), mp)

    def z_at(k):
        return (lax.rem(z + k, n_z) * group + in_group, mp)

    x_to = (lax.rem(chip + n_chip + 2 * core - 1, n_chip) * 2 + 1 - core, mp)

    pending = []

    def remote(src, dst, s_sem, r_sem, device):
        return pltpu.make_async_remote_copy(
            src_ref=src,
            dst_ref=dst,
            send_sem=s_sem,
            recv_sem=r_sem,
            device_id=device,
            device_id_type=MESH,
        )

    def send(*args):
        copy = remote(*args)
        copy.start()
        pending.append(copy)

    loads = []
    own_rows = attn_out.at[mp]
    for n, (src, dst) in enumerate(
        (
            (embedded_h, emb),
            (wk_h, wk),
            (wv_h, wv),
            (attn_out_h, own_rows),
            (wq_h, wq),
            (wr_h, wr),
            (wup_h, wup),
            (wdown_h, wdown),
            (wvocab_h, wvocab),
        )
    ):
        copy = pltpu.make_async_copy(src, dst, load_sem.at[n])
        copy.start()
        loads.append(copy)

    barrier = pltpu.get_barrier_semaphore()
    friends = [partner, forward, backward, x_to]
    friends += [mp_at(k) for k in range(1, N_MP)]
    friends += [group_at(k) for k in range(1, group)]
    friends += [z_at(k) for k in range(1, n_z)]
    for friend in friends:
        pl.semaphore_signal(barrier, inc=1, device_id=friend, device_id_type=MESH)

    def kv_sends(t):
        send(kv_own.at[t], kv_same.at[t], same_s.at[t], same_r.at[t], forward)
        send(kv_own.at[t], kv_partner.at[t], partner_s.at[t], partner_r.at[t], partner)

        @pl.when(core == 0)
        def _():
            remote(kv_own.at[t], kv_x.at[t], x_s.at[t], x_r.at[t], x_to).start()

    loads[0].wait()
    loads[1].wait()
    for t in range(2):
        kv_own[t] = dot(emb[t * HALF : (t + 1) * HALF, :], wk[...]).astype(BF16)
    pl.semaphore_wait(barrier, len(friends))
    for t in range(2):
        kv_sends(t)
    loads[2].wait()
    for t in range(2):
        kv_own[2 + t] = dot(emb[t * HALF : (t + 1) * HALF, :], wv[...]).astype(BF16)
    for t in range(2, 4):
        kv_sends(t)

    loads[3].wait()
    part = pl.ds(pl.multiple_of(core * BLOCK, BLOCK), BLOCK)
    for k in range(1, N_MP):
        here = attn_out.at[mp, part]
        send(here, here, ao_s.at[k - 1], ao_r.at[k - 1], mp_at(k))

    loads[4].wait()
    for t in range(2):
        rows = slice(t * HALF, (t + 1) * HALF)
        q = dot(emb[rows, :], wq[...])
        for h in range(HEADS):
            cols = slice(h * 64, (h + 1) * 64)
            qc[rows, cols] = (q[:, cols] + content_bias[h : h + 1, :]).astype(BF16)
            qp[rows, cols] = (q[:, cols] + position_bias[h : h + 1, :]).astype(BF16)

    loads[5].wait()
    rel[WIDTH:, :] = jnp.zeros((BLOCK, HALF), BF16)

    def rel_block(n, carry):
        for k in range(HALF // FINE):
            at = n * (HALF // FINE) + k
            sin_a, cos_a = basis[0, pl.ds(at, 1), :], basis[1, pl.ds(at, 1), :]
            sin_b, cos_b = basis[2], basis[3]
            rows = slice(k * FINE, (k + 1) * FINE)
            table[rows, : WIDTH // 2] = (sin_a * cos_b + cos_a * sin_b).astype(BF16)
            table[rows, WIDTH // 2 :] = (cos_a * cos_b - sin_a * sin_b).astype(BF16)
        rel[pl.ds(pl.multiple_of(n * HALF, HALF), HALF), :] = dot(table[...], wr[...]).astype(BF16)
        return carry

    lax.fori_loop(0, WIDTH // HALF, rel_block, 0)

    lanes = lax.broadcasted_iota(jnp.int32, (BLOCK, HALF), 1)
    row_at = lax.broadcasted_iota(jnp.int32, (BLOCK, BLOCK), 0)
    col_at = lax.broadcasted_iota(jnp.int32, (BLOCK, BLOCK), 1)

    def of_head(h):
        return (lanes >= h * 64) & (lanes < h * 64 + 64)

    def one_head(ref, rows, mine):
        values = ref[rows, :].astype(F32) * 0.125
        return jnp.where(mine, values, 0.0).astype(BF16)

    def relay(t):
        remote(kv_own.at[t], kv_same.at[t], same_s.at[t], same_r.at[t], forward).wait_recv()
        send(kv_same.at[t], kv_cross.at[t], cross_s.at[t], cross_r.at[t], partner)

        @pl.when(core == 1)
        def _():
            remote(kv_same.at[t], kv_x.at[t], x_s.at[t], x_r.at[t], x_to).start()

    for b in range(ROWS // BLOCK):
        rows = slice(b * BLOCK, (b + 1) * BLOCK)
        own = (b + 1) * BLOCK
        begin = ROWS - own
        width = WIDTH + BLOCK - begin

        def own_part(h, carry, rows=rows, own=own, begin=begin, width=width):
            mine = of_head(h)
            near = dot_t(one_head(qp, rows, mine), rel[begin:, :])
            near = pltpu.roll(near, width - BLOCK + 1, 1, stride=1, stride_axis=0)
            pos_past[h, rows, :] = near[:, :ROWS]
            keys = []
            for c in range(2):
                if own > c * HALF:
                    keys.append(kv_own[c, : min(HALF, own - c * HALF), :])
            query = one_head(qc, rows, mine)
            content = [dot_t(query, piece) for piece in keys]
            content = content[0] if len(content) == 1 else jnp.concatenate(content, axis=1)
            score = content + near[:, ROWS : ROWS + own]
            last = jnp.where(col_at <= row_at, score[:, own - BLOCK :], MASKED)
            score = last if own == BLOCK else jnp.concatenate([score[:, : own - BLOCK], last], axis=1)
            top = jnp.max(score, axis=-1, keepdims=True)
            weight = jnp.exp(score - top)
            top_own[h, rows, :] = top
            sum_own[h, rows, :] = jnp.sum(weight, axis=-1, keepdims=True)
            weight = weight.astype(BF16)
            total = None
            for c, piece in enumerate(keys):
                n = piece.shape[0]
                term = dot(weight[:, c * HALF : c * HALF + n], kv_own[2 + c, :n, :])
                total = term if total is None else total + term
            out_own[rows, :] = jnp.where(mine, total, out_own[rows, :])
            return carry

        out_own[rows, :] = jnp.zeros((BLOCK, HALF), F32)
        lax.fori_loop(0, HEADS, own_part, 0)
        relay(b)

    for k in range(1, N_MP):
        there = lax.rem(mp + N_MP - k, N_MP)
        here = attn_out.at[there, part]
        remote(here, here, ao_s.at[k - 1], ao_r.at[k - 1], mp_at(k)).wait_recv()
        send(here, here, aof_s.at[k - 1], aof_r.at[k - 1], partner)

    behind = seg - pred_s[0]
    has_memory = pred_s[0] >= 0
    use_cross = behind == 1 + 2 * core
    use_partner = behind == 2 * core - 1
    use_x = behind == 3 - 4 * core
    for t in range(4):
        remote(kv_own.at[t], kv_partner.at[t], partner_s.at[t], partner_r.at[t], partner).wait_recv()
        remote(kv_same.at[t], kv_cross.at[t], cross_s.at[t], cross_r.at[t], partner).wait_recv()
        remote(kv_same.at[t], kv_x.at[t], x_s.at[t], x_r.at[t], x_to).wait_recv()
        chosen = jnp.where(use_cross, kv_cross[t], kv_same[t])
        chosen = jnp.where(use_partner, kv_partner[t], chosen)
        kv_past[t] = jnp.where(use_x, kv_x[t], chosen)

    for b in range(ROWS // BLOCK):
        rows = slice(b * BLOCK, (b + 1) * BLOCK)

        def past_part(h, carry, rows=rows):
            mine = of_head(h)
            query = one_head(qc, rows, mine)
            score = jnp.concatenate([dot_t(query, kv_past[c]) for c in range(2)], axis=1)
            score = jnp.where(has_memory, score + pos_past[h, rows, :], MASKED)
            before = top_own[h, rows, :]
            top = jnp.maximum(before, jnp.max(score, axis=-1, keepdims=True))
            weight = jnp.exp(score - top)
            fade = jnp.exp(before - top)
            total = sum_own[h, rows, :] * fade + jnp.sum(weight, axis=-1, keepdims=True)
            weight = weight.astype(BF16)
            past = dot(weight[:, :HALF], kv_past[2]) + dot(weight[:, HALF:], kv_past[3])
            done = (out_own[rows, :] * fade + past) / total
            att_acc[...] = jnp.where(mine, done, att_acc[...])
            return carry

        att_acc[...] = jnp.zeros((BLOCK, HALF), F32)
        lax.fori_loop(0, HEADS, past_part, 0)
        attended[mp, rows, :] = att_acc[...].astype(BF16)
        for k in range(1, N_MP):
            here = attended.at[mp, rows]
            send(here, here, att_s.at[k - 1, b], att_r.at[k - 1, b], mp_at(k))

    for k in range(1, N_MP):
        there = lax.rem(mp + N_MP - k, N_MP)
        other = pl.ds(pl.multiple_of((1 - core) * BLOCK, BLOCK), BLOCK)
        here = attn_out.at[there, other]
        remote(here, here, aof_s.at[k - 1], aof_r.at[k - 1], partner).wait_recv()
    loads[6].wait()
    loads[7].wait()
    loads[8].wait()

    for half in range(2):
        rows = slice(half * HALF, (half + 1) * HALF)
        for b in range(2 * half, 2 * half + 2):
            for k in range(1, N_MP):
                there = lax.rem(mp + N_MP - k, N_MP)
                here = attended.at[there, b * BLOCK : (b + 1) * BLOCK]
                remote(here, here, att_s.at[k - 1, b], att_r.at[k - 1, b], mp_at(k)).wait_recv()
        total = emb[rows, :].astype(F32)
        head_sum = None
        for g in range(N_MP):
            term = dot(attended[g, rows, :], attn_out[g]).astype(BF16).astype(F32)
            head_sum = term if head_sum is None else head_sum + term
        first = normalize(total + head_sum, attn_gain[...], attn_shift[...]).astype(BF16)
        first_out[rows, :] = first
        units[...] = jnp.maximum(dot(first, wup[...]) + up_bias[...], 0.0).astype(BF16)
        terms = dot(units[...], wdown[...]).astype(BF16)
        for d in range(N_MP):
            rs_send[half, d] = terms[d * PIECE : (d + 1) * PIECE, :]
        for k in range(1, N_MP):
            to = lax.rem(mp + k, N_MP)
            send(rs_send.at[half, to], rs_recv.at[half, k - 1], rs_s.at[k - 1, half], rs_r.at[k - 1, half], mp_at(k))

    for half in range(2):
        total = rs_send[half, mp].astype(F32)
        for k in range(1, N_MP):
            to = lax.rem(mp + k, N_MP)
            remote(rs_send.at[half, to], rs_recv.at[half, k - 1], rs_s.at[k - 1, half], rs_r.at[k - 1, half], mp_at(k)).wait_recv()
            total = total + rs_recv[half, k - 1].astype(F32)
        at = pl.ds(pl.multiple_of(half * HALF + mp * PIECE, PIECE), PIECE)
        total = first_out[at, :].astype(F32) + total + down_bias[...]
        second[half, mp] = normalize(total, ffn_gain[...], ffn_shift[...]).astype(BF16)
        for k in range(1, N_MP):
            here = second.at[half, mp]
            send(here, here, ag_s.at[k - 1, half], ag_r.at[k - 1, half], mp_at(k))

    tile = 512
    n_words = wvocab_h.shape[1]
    for half in range(2):
        rows = slice(half * HALF, (half + 1) * HALF)
        for k in range(1, N_MP):
            there = lax.rem(mp + N_MP - k, N_MP)
            here = second.at[half, there]
            remote(here, here, ag_s.at[k - 1, half], ag_r.at[k - 1, half], mp_at(k)).wait_recv()
        states = jnp.concatenate([second[half, d] for d in range(N_MP)], axis=0)
        wanted = targets[rows, :] - mp * n_words
        words = lax.broadcasted_iota(jnp.int32, (HALF, tile), 1)

        def vocab_tile(n, carry, states=states, wanted=wanted, words=words):
            top, total, picked = carry
            at = pl.multiple_of(n * tile, tile)
            logits = dot(states, wvocab[:, pl.ds(at, tile)])
            new_top = jnp.maximum(top, jnp.max(logits, axis=1, keepdims=True))
            total = total * jnp.exp(top - new_top)
            total = total + jnp.sum(jnp.exp(logits - new_top), axis=1, keepdims=True)
            hit = jnp.where(words == wanted - at, logits, 0.0)
            return new_top, total, picked + jnp.sum(hit, axis=1, keepdims=True)

        zero = jnp.zeros((HALF, 1), F32)
        top, total, picked = lax.fori_loop(
            0, n_words // tile, vocab_tile, (jnp.full((HALF, 1), -jnp.inf, F32), zero, zero)
        )
        lane = lax.broadcasted_iota(jnp.int32, (HALF, BLOCK), 1)
        packed = jnp.where(lane == 0, top, jnp.where(lane == 1, total, picked))
        stats[mp, :, rows] = jnp.transpose(packed)[:8, :]

    for k in range(1, N_MP):
        here = stats.at[mp]
        send(here, here, st_s.at[k - 1], st_r.at[k - 1], mp_at(k))
    for k in range(1, N_MP):
        there = lax.rem(mp + N_MP - k, N_MP)
        here = stats.at[there]
        remote(here, here, st_s.at[k - 1], st_r.at[k - 1], mp_at(k)).wait_recv()
    top = stats[0, 0:1, :]
    for g in range(1, N_MP):
        top = jnp.maximum(top, stats[g, 0:1, :])
    total, picked = None, None
    for g in range(N_MP):
        term = stats[g, 1:2, :] * jnp.exp(stats[g, 0:1, :] - top)
        total = term if total is None else total + term
        picked = stats[g, 2:3, :] if picked is None else picked + stats[g, 2:3, :]
    position = lax.broadcasted_iota(jnp.int32, (1, ROWS), 1)
    tokens = jnp.where(position < valid_s[0], picked - (top + jnp.log(total)), 0.0)
    token_o[...] = tokens

    slot = lax.broadcasted_iota(jnp.int32, (8, BLOCK), 1) == doc_s[0]
    line = lax.broadcasted_iota(jnp.int32, (8, BLOCK), 0)
    used = valid_s[0].astype(F32)
    share = jnp.sum(tokens, axis=1, keepdims=True)
    doc_a[0] = jnp.where(slot, jnp.where(line == 0, share, jnp.where(line == 1, used, 0.0)), 0.0)
    for k in range(1, group):
        send(doc_a.at[0], doc_a.at[k], da_s.at[k - 1], da_r.at[k - 1], group_at(k))
    for k in range(1, group):
        remote(doc_a.at[0], doc_a.at[k], da_s.at[k - 1], da_r.at[k - 1], group_at(k)).wait_recv()
    doc_b[0] = jnp.sum(doc_a[...], axis=0)
    for k in range(1, n_z):
        send(doc_b.at[0], doc_b.at[k], db_s.at[k - 1], db_r.at[k - 1], z_at(k))
    for k in range(1, n_z):
        remote(doc_b.at[0], doc_b.at[k], db_s.at[k - 1], db_r.at[k - 1], z_at(k)).wait_recv()
    docs = jnp.sum(doc_b[...], axis=0)
    doc_o[...] = docs[0:1, :] / docs[1:2, :]

    for copy in pending:
        copy.wait_send()
    for t in range(4):
        remote(kv_own.at[t], kv_x.at[t], x_s.at[t], x_r.at[t], x_to).wait_send()


def angle_basis():
    frequency = 10000.0 ** (-np.arange(0, WIDTH, 2, dtype=np.float64) / WIDTH)
    coarse = (WIDTH // FINE - 1 - np.arange(WIDTH // FINE))[:, None] * FINE * frequency[None, :]
    fine = (FINE - 1 - np.arange(FINE))[:, None] * frequency[None, :]
    return np.stack([np.sin(coarse), np.cos(coarse), np.sin(fine), np.cos(fine)]).astype(np.float32)


def on_device(
    n_seg,
    embedded,
    targets,
    pred_device,
    doc_ids,
    valid_rows,
    w_query,
    w_key,
    w_value,
    w_rel,
    content_bias,
    position_bias,
    attn_out,
    attn_gain,
    attn_shift,
    w_up,
    up_bias,
    w_down,
    down_bias,
    ffn_gain,
    ffn_shift,
    w_vocab,
):
    smem = pl.BlockSpec(memory_space=pltpu.SMEM)
    vmem = pl.BlockSpec(memory_space=pltpu.VMEM)
    hbm = pl.BlockSpec(memory_space=pl.ANY)
    dma = pltpu.SemaphoreType.DMA
    words = w_vocab.shape[1]
    n_z = n_seg // (2 * N_X)
    kv = pltpu.VMEM((4, HALF, HALF), BF16)
    weight = pltpu.VMEM((WIDTH, HALF), BF16)
    column = pltpu.VMEM((HEADS, ROWS, 1), F32)
    scratch = [
        pltpu.VMEM((ROWS, WIDTH), BF16),
        weight,
        weight,
        weight,
        weight,
        pltpu.VMEM((N_MP, HALF, WIDTH), BF16),
        pltpu.VMEM((WIDTH, WIDTH), BF16),
        pltpu.VMEM((WIDTH, WIDTH), BF16),
        pltpu.VMEM((WIDTH, words), BF16),
        pltpu.VMEM((HALF, WIDTH), BF16),
        pltpu.VMEM((WIDTH + BLOCK, HALF), BF16),
        pltpu.VMEM((ROWS, HALF), BF16),
        pltpu.VMEM((ROWS, HALF), BF16),
        kv,
        kv,
        kv,
        kv,
        kv,
        kv,
        pltpu.VMEM((HEADS, ROWS, ROWS), F32),
        column,
        column,
        pltpu.VMEM((ROWS, HALF), F32),
        pltpu.VMEM((BLOCK, HALF), F32),
        pltpu.VMEM((N_MP, ROWS, HALF), BF16),
        pltpu.VMEM((ROWS, WIDTH), BF16),
        pltpu.VMEM((HALF, WIDTH), BF16),
        pltpu.VMEM((2, N_MP, PIECE, WIDTH), BF16),
        pltpu.VMEM((2, N_MP - 1, PIECE, WIDTH), BF16),
        pltpu.VMEM((2, N_MP, PIECE, WIDTH), BF16),
        pltpu.VMEM((8, BLOCK), F32),
        pltpu.VMEM((N_MP, 8, ROWS), F32),
        pltpu.VMEM((2 * N_X, 8, BLOCK), F32),
        pltpu.VMEM((n_z, 8, BLOCK), F32),
        dma((9,)),
    ]
    scratch += [dma((4,))] * 8
    scratch += [dma((N_MP - 1,))] * 4
    scratch += [dma((N_MP - 1, 4))] * 2
    scratch += [dma((N_MP - 1, 2))] * 4
    scratch += [dma((N_MP - 1,))] * 2
    scratch += [dma((2 * N_X - 1,))] * 2
    scratch += [dma((n_z - 1,))] * 2
    token_terms, docs = pl.pallas_call(
        functools.partial(kernel, n_seg),
        out_shape=(
            jax.ShapeDtypeStruct((1, ROWS), F32),
            jax.ShapeDtypeStruct((1, BLOCK), F32),
        ),
        in_specs=[smem] * 3 + [vmem] * 10 + [hbm] * 9,
        out_specs=(vmem, vmem),
        scratch_shapes=scratch,
        compiler_params=pltpu.CompilerParams(
            collective_id=0, has_side_effects=True, vmem_limit_bytes=60 * 1024 * 1024
        ),
        name="layer",
    )(
        pred_device,
        doc_ids,
        valid_rows,
        content_bias,
        position_bias,
        jnp.asarray(angle_basis()),
        targets.reshape(ROWS, 1),
        attn_gain.reshape(1, WIDTH),
        attn_shift.reshape(1, WIDTH),
        up_bias.reshape(1, WIDTH),
        down_bias.reshape(1, WIDTH),
        ffn_gain.reshape(1, WIDTH),
        ffn_shift.reshape(1, WIDTH),
        embedded,
        w_query,
        w_key,
        w_value,
        w_rel,
        attn_out,
        w_up,
        w_down,
        w_vocab,
    )
    doc_slots = n_seg // 4
    return token_terms.reshape(ROWS), docs[0, :doc_slots]


def solution(mesh):
    return jax.shard_map(
        functools.partial(on_device, mesh.shape["seg"]),
        mesh=mesh,
        in_specs=(
            P("seg", None),
            P("seg"),
            P("seg"),
            P("seg"),
            P("seg"),
            P(None, "mp"),
            P(None, "mp"),
            P(None, "mp"),
            P(None, "mp"),
            P("mp", None),
            P("mp", None),
            P("mp", None),
            P(),
            P(),
            P(None, "mp"),
            P("mp"),
            P("mp", None),
            P(),
            P(),
            P(),
            P(None, "mp"),
        ),
        out_specs=(P("seg"), P()),
        check_vma=False,
    )
```

profile of v0, /device:TPU:4, one launch (start us, length us, event | category | flops | bytes accessed | tf_op | source)
XLA Modules:
  0.0 90.0 jit_solution(18217551479192643683)
XLA Ops:
  2.6 1.5 %copy.24.targets = s32[512,1]{1,0:T(8,128)} copy(s32[512,1]{0,1:T(1,128)} %bitcast.16) | data formatting | bytes 4096 | tf_op jit(solution)/shard_map/reshape | solution.py:572
  4.1 83.6 %layer.1 = (f32[1,512]{1,0:T(1,128)}, f32[1,128]{1,0:T(1,128)}) custom-call(s32[1]{0:T(128)S(6)} %copy.26.pred_s, s32[1]{0:T(128)S(6)} %copy.27.doc_s, s32[1]{0:T(128)S(6)} %copy.28.valid_s, f32[4,64]{1,0:T(4,128)} %content_bias.1, f32[4,64]{1,0:T(4,128)} %position_bias.1, f32[4,32,512]{2,1,0:T(8,128)} %constant.2.clone.basis, s32[512,1]{1,0:T(8,128)} %copy.24.targets, ...), custom_call_target="tpu_custom_call" | custom-call | tf_op jit(solution)/shard_map/layer/pallas_call | solution.py:552
  87.7 1.1 %slice_bitcast_fusion = f32[16]{0:T(128)} fusion(f32[1,128]{1,0:T(1,128)} %get-tuple-element.5), kind=kLoop, calls=%fused_computation | loop fusion | bytes 128 | tf_op jit(solution)/shard_map/squeeze | solution.py:590
  88.8 1.2 %copy.29 = f32[512]{0:T(512)} copy(f32[512]{0:T(512)} %bitcast.17) | data formatting | bytes 4096
where the time goes:
time: 90.2 us; the launch traced here: 90 us
  Pallas kernels  83.6 us (93%)
  local copies, waits for them, and re-layouts  3.86 us (4%)
  between operations  2.58 us (3%)
    pallas_call x1, Pallas kernels, on_device(): pl.pallas_call(functools.partial(kernel, n_seg), out_shape=(jax.ShapeDtyp...  83.6 us

commit v1 on v0

--- a/solution.py
+++ b/solution.py
@@ -39,19 +39,19 @@
 
 def kernel(
     n_seg,
-    pred_s,
-    doc_s,
-    valid_s,
-    content_bias,
-    position_bias,
-    basis,
-    targets,
-    attn_gain,
-    attn_shift,
-    up_bias,
-    down_bias,
-    ffn_gain,
-    ffn_shift,
+    pred_v,
+    doc_v,
+    valid_v,
+    content_bias_h,
+    position_bias_h,
+    basis_h,
+    targets_h,
+    attn_gain_h,
+    attn_shift_h,
+    up_bias_h,
+    down_bias_h,
+    ffn_gain_h,
+    ffn_shift_h,
     embedded_h,
     wq_h,
     wk_h,
@@ -63,6 +63,16 @@
     wvocab_h,
     token_o,
     doc_o,
+    content_bias,
+    position_bias,
+    basis,
+    targets,
+    attn_gain,
+    attn_shift,
+    up_bias,
+    down_bias,
+    ffn_gain,
+    ffn_shift,
     emb,
     wq,
     wk,
@@ -86,14 +96,14 @@
     top_own,
     sum_own,
     out_own,
-    att_acc,
     attended,
     first_out,
     units,
     rs_send,
     rs_recv,
+    rs_pass,
     second,
-    stats_col,
+    target_col,
     stats,
     doc_a,
     doc_b,
@@ -168,24 +178,30 @@
         copy.start()
         pending.append(copy)
 
-    loads = []
-    own_rows = attn_out.at[mp]
-    for n, (src, dst) in enumerate(
-        (
-            (embedded_h, emb),
-            (wk_h, wk),
-            (wv_h, wv),
-            (attn_out_h, own_rows),
-            (wq_h, wq),
-            (wr_h, wr),
-            (wup_h, wup),
-            (wdown_h, wdown),
-            (wvocab_h, wvocab),
-        )
-    ):
-        copy = pltpu.make_async_copy(src, dst, load_sem.at[n])
-        copy.start()
-        loads.append(copy)
+    sources = (
+        (embedded_h, emb),
+        (wk_h, wk),
+        (wv_h, wv),
+        (attn_out_h, attn_out.at[mp]),
+        (wq_h, wq),
+        (wr_h, wr),
+        (wup_h, wup),
+        (wdown_h, wdown),
+        (wvocab_h, wvocab),
+        (content_bias_h, content_bias),
+        (position_bias_h, position_bias),
+        (basis_h, basis),
+        (targets_h, targets),
+        (attn_gain_h, attn_gain),
+        (attn_shift_h, attn_shift),
+        (up_bias_h, up_bias),
+        (down_bias_h, down_bias),
+        (ffn_gain_h, ffn_gain),
+        (ffn_shift_h, ffn_shift),
+    )
+    loads = [pltpu.make_async_copy(src, dst, load_sem.at[n]) for n, (src, dst) in enumerate(sources)]
+    for n in (0, 1, 2, 4, 9, 10, 11, 5, 3, *range(12, 19)):
+        loads[n].start()
 
     barrier = pltpu.get_barrier_semaphore()
     friends = [partner, forward, backward, x_to]
@@ -217,12 +233,16 @@
         kv_sends(t)
 
     loads[3].wait()
+    for n in (6, 7, 8):
+        loads[n].start()
     part = pl.ds(pl.multiple_of(core * BLOCK, BLOCK), BLOCK)
     for k in range(1, N_MP):
         here = attn_out.at[mp, part]
         send(here, here, ao_s.at[k - 1], ao_r.at[k - 1], mp_at(k))
 
     loads[4].wait()
+    loads[9].wait()
+    loads[10].wait()
     for t in range(2):
         rows = slice(t * HALF, (t + 1) * HALF)
         q = dot(emb[rows, :], wq[...])
@@ -232,6 +252,7 @@
             qp[rows, cols] = (q[:, cols] + position_bias[h : h + 1, :]).astype(BF16)
 
     loads[5].wait()
+    loads[11].wait()
     rel[WIDTH:, :] = jnp.zeros((BLOCK, HALF), BF16)
 
     def rel_block(n, carry):
@@ -272,17 +293,18 @@
         begin = ROWS - own
         width = WIDTH + BLOCK - begin
 
-        def own_part(h, carry, rows=rows, own=own, begin=begin, width=width):
+        keys = []
+        for c in range(2):
+            if own > c * HALF:
+                keys.append((c, min(HALF, own - c * HALF)))
+        outcome = None
+        for h in range(HEADS):
             mine = of_head(h)
             near = dot_t(one_head(qp, rows, mine), rel[begin:, :])
             near = pltpu.roll(near, width - BLOCK + 1, 1, stride=1, stride_axis=0)
             pos_past[h, rows, :] = near[:, :ROWS]
-            keys = []
-            for c in range(2):
-                if own > c * HALF:
-                    keys.append(kv_own[c, : min(HALF, own - c * HALF), :])
             query = one_head(qc, rows, mine)
-            content = [dot_t(query, piece) for piece in keys]
+            content = [dot_t(query, kv_own[c, :n, :]) for c, n in keys]
             content = content[0] if len(content) == 1 else jnp.concatenate(content, axis=1)
             score = content + near[:, ROWS : ROWS + own]
             last = jnp.where(col_at <= row_at, score[:, own - BLOCK :], MASKED)
@@ -293,15 +315,11 @@
             sum_own[h, rows, :] = jnp.sum(weight, axis=-1, keepdims=True)
             weight = weight.astype(BF16)
             total = None
-            for c, piece in enumerate(keys):
-                n = piece.shape[0]
+            for c, n in keys:
                 term = dot(weight[:, c * HALF : c * HALF + n], kv_own[2 + c, :n, :])
                 total = term if total is None else total + term
-            out_own[rows, :] = jnp.where(mine, total, out_own[rows, :])
-            return carry
-
-        out_own[rows, :] = jnp.zeros((BLOCK, HALF), F32)
-        lax.fori_loop(0, HEADS, own_part, 0)
+            outcome = total if outcome is None else jnp.where(mine, total, outcome)
+        out_own[rows, :] = outcome
         relay(b)
 
     for k in range(1, N_MP):
@@ -310,8 +328,13 @@
         remote(here, here, ao_s.at[k - 1], ao_r.at[k - 1], mp_at(k)).wait_recv()
         send(here, here, aof_s.at[k - 1], aof_r.at[k - 1], partner)
 
-    behind = seg - pred_s[0]
-    has_memory = pred_s[0] >= 0
+    for n in range(12, 19):
+        loads[n].wait()
+    spread = jnp.broadcast_to(targets[...].astype(F32), (BLOCK, ROWS))
+    target_col[...] = jnp.transpose(spread)[:, :8]
+    previous = pred_v[...]
+    behind = jnp.broadcast_to(seg - previous, (HALF, HALF))
+    has_memory = jnp.broadcast_to(previous, (BLOCK, ROWS)) >= 0
     use_cross = behind == 1 + 2 * core
     use_partner = behind == 2 * core - 1
     use_x = behind == 3 - 4 * core
@@ -323,10 +346,27 @@
         chosen = jnp.where(use_partner, kv_partner[t], chosen)
         kv_past[t] = jnp.where(use_x, kv_x[t], chosen)
 
+    side = (mp_at(1), mp_at(N_MP - 1))
+    source = (lax.rem(mp + N_MP - 1, N_MP), lax.rem(mp + 1, N_MP))
+    across = lax.rem(mp + 2, N_MP)
+
+    def pass_attended(b):
+        for k in range(2):
+            here = attended.at[source[k], b * BLOCK : (b + 1) * BLOCK]
+            remote(here, here, att_s.at[k, b], att_r.at[k, b], side[k]).wait_recv()
+            here = attended.at[source[k], b * BLOCK + k * PIECE : b * BLOCK + (k + 1) * PIECE]
+            send(here, here, att_s.at[2 + k, b], att_r.at[2 + k, b], side[k])
+
+    def attended_arrived(b):
+        for k in range(2):
+            here = attended.at[across, b * BLOCK + k * PIECE : b * BLOCK + (k + 1) * PIECE]
+            remote(here, here, att_s.at[2 + k, b], att_r.at[2 + k, b], side[k]).wait_recv()
+
     for b in range(ROWS // BLOCK):
         rows = slice(b * BLOCK, (b + 1) * BLOCK)
 
-        def past_part(h, carry, rows=rows):
+        outcome = None
+        for h in range(HEADS):
             mine = of_head(h)
             query = one_head(qc, rows, mine)
             score = jnp.concatenate([dot_t(query, kv_past[c]) for c in range(2)], axis=1)
@@ -339,15 +379,13 @@
             weight = weight.astype(BF16)
             past = dot(weight[:, :HALF], kv_past[2]) + dot(weight[:, HALF:], kv_past[3])
             done = (out_own[rows, :] * fade + past) / total
-            att_acc[...] = jnp.where(mine, done, att_acc[...])
-            return carry
-
-        att_acc[...] = jnp.zeros((BLOCK, HALF), F32)
-        lax.fori_loop(0, HEADS, past_part, 0)
-        attended[mp, rows, :] = att_acc[...].astype(BF16)
-        for k in range(1, N_MP):
-            here = attended.at[mp, rows]
-            send(here, here, att_s.at[k - 1, b], att_r.at[k - 1, b], mp_at(k))
+            outcome = done if outcome is None else jnp.where(mine, done, outcome)
+        attended[mp, rows, :] = outcome.astype(BF16)
+        here = attended.at[mp, rows]
+        for k in range(2):
+            send(here, here, att_s.at[k, b], att_r.at[k, b], side[k])
+        if b > 0:
+            pass_attended(b - 1)
 
     for k in range(1, N_MP):
         there = lax.rem(mp + N_MP - k, N_MP)
@@ -358,13 +396,38 @@
     loads[7].wait()
     loads[8].wait()
 
+    part_rows = (slice(0, PIECE // 2), slice(PIECE // 2, PIECE))
+
+    def reduce_copy(half, n):
+        k = n % 2
+        if n < 2:
+            src = rs_send.at[half, source[1 - k], part_rows[1 - k]]
+        elif n < 4:
+            src = rs_pass.at[half, k]
+        else:
+            src = rs_send.at[half, across, part_rows[k]]
+        return remote(src, rs_recv.at[half, n], rs_s.at[n, half], rs_r.at[n, half], side[k])
+
+    def start_reduce(half, n):
+        copy = reduce_copy(half, n)
+        copy.start()
+        pending.append(copy)
+
+    def pass_reduce(half):
+        for k in range(2):
+            reduce_copy(half, 4 + k).wait_recv()
+            mine = rs_send[half, source[1 - k], part_rows[k]].astype(F32)
+            rs_pass[half, k] = (mine + rs_recv[half, 4 + k].astype(F32)).astype(BF16)
+            start_reduce(half, 2 + k)
+
     for half in range(2):
         rows = slice(half * HALF, (half + 1) * HALF)
-        for b in range(2 * half, 2 * half + 2):
-            for k in range(1, N_MP):
-                there = lax.rem(mp + N_MP - k, N_MP)
-                here = attended.at[there, b * BLOCK : (b + 1) * BLOCK]
-                remote(here, here, att_s.at[k - 1, b], att_r.at[k - 1, b], mp_at(k)).wait_recv()
+        if half == 1:
+            attended_arrived(2)
+            attended_arrived(3)
+        else:
+            attended_arrived(0)
+            attended_arrived(1)
         total = emb[rows, :].astype(F32)
         head_sum = None
         for g in range(N_MP):
@@ -372,37 +435,67 @@
             head_sum = term if head_sum is None else head_sum + term
         first = normalize(total + head_sum, attn_gain[...], attn_shift[...]).astype(BF16)
         first_out[rows, :] = first
+        if half == 0:
+            pass_attended(3)
         units[...] = jnp.maximum(dot(first, wup[...]) + up_bias[...], 0.0).astype(BF16)
+        if half == 1:
+            pass_reduce(0)
         terms = dot(units[...], wdown[...]).astype(BF16)
         for d in range(N_MP):
             rs_send[half, d] = terms[d * PIECE : (d + 1) * PIECE, :]
-        for k in range(1, N_MP):
-            to = lax.rem(mp + k, N_MP)
-            send(rs_send.at[half, to], rs_recv.at[half, k - 1], rs_s.at[k - 1, half], rs_r.at[k - 1, half], mp_at(k))
-
-    for half in range(2):
-        total = rs_send[half, mp].astype(F32)
-        for k in range(1, N_MP):
-            to = lax.rem(mp + k, N_MP)
-            remote(rs_send.at[half, to], rs_recv.at[half, k - 1], rs_s.at[k - 1, half], rs_r.at[k - 1, half], mp_at(k)).wait_recv()
-            total = total + rs_recv[half, k - 1].astype(F32)
-        at = pl.ds(pl.multiple_of(half * HALF + mp * PIECE, PIECE), PIECE)
-        total = first_out[at, :].astype(F32) + total + down_bias[...]
-        second[half, mp] = normalize(total, ffn_gain[...], ffn_shift[...]).astype(BF16)
-        for k in range(1, N_MP):
+        for n in (4, 5, 0, 1):
+            start_reduce(half, n)
+
+    def second_copy(half, n):
+        k = n % 2
+        if n < 2:
             here = second.at[half, mp]
-            send(here, here, ag_s.at[k - 1, half], ag_r.at[k - 1, half], mp_at(k))
+        else:
+            here = second.at[half, source[k], part_rows[k]]
+        return remote(here, here, ag_s.at[n, half], ag_r.at[n, half], side[k])
+
+    def start_second(half, n):
+        copy = second_copy(half, n)
+        copy.start()
+        pending.append(copy)
+
+    def pass_second(half):
+        for k in range(2):
+            here = second.at[half, source[k]]
+            remote(here, here, ag_s.at[k, half], ag_r.at[k, half], side[k]).wait_recv()
+            start_second(half, 2 + k)
+
+    def second_arrived(half):
+        for k in range(2):
+            here = second.at[half, across, part_rows[k]]
+            remote(here, here, ag_s.at[2 + k, half], ag_r.at[2 + k, half], side[k]).wait_recv()
+
+    def finish_reduce(half):
+        for n in range(4):
+            reduce_copy(half, n).wait_recv()
+        for k in range(2):
+            total = rs_send[half, mp, part_rows[k]].astype(F32)
+            total = total + rs_recv[half, 1 - k].astype(F32) + rs_recv[half, 2 + k].astype(F32)
+            start = half * HALF + mp * PIECE + k * (PIECE // 2)
+            at = pl.ds(pl.multiple_of(start, PIECE // 2), PIECE // 2)
+            total = first_out[at, :].astype(F32) + total + down_bias[...]
+            total = normalize(total, ffn_gain[...], ffn_shift[...]).astype(BF16)
+            second[half, mp, part_rows[k]] = total
+        for n in range(2):
+            start_second(half, n)
+
+    finish_reduce(0)
+    pass_reduce(1)
+    pass_second(0)
+    finish_reduce(1)
 
     tile = 512
     n_words = wvocab_h.shape[1]
     for half in range(2):
         rows = slice(half * HALF, (half + 1) * HALF)
-        for k in range(1, N_MP):
-            there = lax.rem(mp + N_MP - k, N_MP)
-            here = second.at[half, there]
-            remote(here, here, ag_s.at[k - 1, half], ag_r.at[k - 1, half], mp_at(k)).wait_recv()
+        second_arrived(half)
         states = jnp.concatenate([second[half, d] for d in range(N_MP)], axis=0)
-        wanted = targets[rows, :] - mp * n_words
+        wanted = target_col[rows, 0:1].astype(jnp.int32) - mp * n_words
         words = lax.broadcasted_iota(jnp.int32, (HALF, tile), 1)
 
         def vocab_tile(n, carry, states=states, wanted=wanted, words=words):
@@ -416,9 +509,11 @@
             return new_top, total, picked + jnp.sum(hit, axis=1, keepdims=True)
 
         zero = jnp.zeros((HALF, 1), F32)
-        top, total, picked = lax.fori_loop(
-            0, n_words // tile, vocab_tile, (jnp.full((HALF, 1), -jnp.inf, F32), zero, zero)
-        )
+        found = (jnp.full((HALF, 1), -jnp.inf, F32), zero, zero)
+        found = lax.fori_loop(0, 2, vocab_tile, found)
+        if half == 0:
+            pass_second(1)
+        top, total, picked = lax.fori_loop(2, n_words // tile, vocab_tile, found)
         lane = lax.broadcasted_iota(jnp.int32, (HALF, BLOCK), 1)
         packed = jnp.where(lane == 0, top, jnp.where(lane == 1, total, picked))
         stats[mp, :, rows] = jnp.transpose(packed)[:8, :]
@@ -439,12 +534,12 @@
         total = term if total is None else total + term
         picked = stats[g, 2:3, :] if picked is None else picked + stats[g, 2:3, :]
     position = lax.broadcasted_iota(jnp.int32, (1, ROWS), 1)
-    tokens = jnp.where(position < valid_s[0], picked - (top + jnp.log(total)), 0.0)
+    tokens = jnp.where(position < jnp.broadcast_to(valid_v[...], (1, ROWS)), picked - (top + jnp.log(total)), 0.0)
     token_o[...] = tokens
 
-    slot = lax.broadcasted_iota(jnp.int32, (8, BLOCK), 1) == doc_s[0]
+    slot = lax.broadcasted_iota(jnp.int32, (8, BLOCK), 1) == jnp.broadcast_to(doc_v[...], (8, BLOCK))
     line = lax.broadcasted_iota(jnp.int32, (8, BLOCK), 0)
-    used = valid_s[0].astype(F32)
+    used = valid_v[...].astype(F32)
     share = jnp.sum(tokens, axis=1, keepdims=True)
     doc_a[0] = jnp.where(slot, jnp.where(line == 0, share, jnp.where(line == 1, used, 0.0)), 0.0)
     for k in range(1, group):
@@ -463,6 +558,11 @@
         copy.wait_send()
     for t in range(4):
         remote(kv_own.at[t], kv_x.at[t], x_s.at[t], x_r.at[t], x_to).wait_send()
+
+
+def hand_over(token_i, doc_i, token_o, doc_o):
+    token_o[...] = token_i[...]
+    doc_o[...] = doc_i[:, : doc_o.shape[1]]
 
 
 def angle_basis():
@@ -496,16 +596,26 @@
     ffn_shift,
     w_vocab,
 ):
-    smem = pl.BlockSpec(memory_space=pltpu.SMEM)
     vmem = pl.BlockSpec(memory_space=pltpu.VMEM)
-    hbm = pl.BlockSpec(memory_space=pl.ANY)
+    hbm = pl.BlockSpec(memory_space=pltpu.HBM)
     dma = pltpu.SemaphoreType.DMA
     words = w_vocab.shape[1]
     n_z = n_seg // (2 * N_X)
     kv = pltpu.VMEM((4, HALF, HALF), BF16)
     weight = pltpu.VMEM((WIDTH, HALF), BF16)
     column = pltpu.VMEM((HEADS, ROWS, 1), F32)
+    vector = pltpu.VMEM((1, WIDTH), F32)
     scratch = [
+        pltpu.VMEM((HEADS, 64), F32),
+        pltpu.VMEM((HEADS, 64), F32),
+        pltpu.VMEM((4, FINE, WIDTH // 2), F32),
+        pltpu.VMEM((1, ROWS), jnp.int32),
+        vector,
+        vector,
+        vector,
+        vector,
+        vector,
+        vector,
         pltpu.VMEM((ROWS, WIDTH), BF16),
         weight,
         weight,
@@ -529,23 +639,24 @@
         column,
         column,
         pltpu.VMEM((ROWS, HALF), F32),
-        pltpu.VMEM((BLOCK, HALF), F32),
         pltpu.VMEM((N_MP, ROWS, HALF), BF16),
         pltpu.VMEM((ROWS, WIDTH), BF16),
         pltpu.VMEM((HALF, WIDTH), BF16),
         pltpu.VMEM((2, N_MP, PIECE, WIDTH), BF16),
-        pltpu.VMEM((2, N_MP - 1, PIECE, WIDTH), BF16),
+        pltpu.VMEM((2, 6, PIECE // 2, WIDTH), BF16),
+        pltpu.VMEM((2, 2, PIECE // 2, WIDTH), BF16),
         pltpu.VMEM((2, N_MP, PIECE, WIDTH), BF16),
-        pltpu.VMEM((8, BLOCK), F32),
+        pltpu.VMEM((ROWS, 8), F32),
         pltpu.VMEM((N_MP, 8, ROWS), F32),
         pltpu.VMEM((2 * N_X, 8, BLOCK), F32),
         pltpu.VMEM((n_z, 8, BLOCK), F32),
-        dma((9,)),
+        dma((19,)),
     ]
     scratch += [dma((4,))] * 8
     scratch += [dma((N_MP - 1,))] * 4
-    scratch += [dma((N_MP - 1, 4))] * 2
-    scratch += [dma((N_MP - 1, 2))] * 4
+    scratch += [dma((4, 4))] * 2
+    scratch += [dma((6, 2))] * 2
+    scratch += [dma((4, 2))] * 2
     scratch += [dma((N_MP - 1,))] * 2
     scratch += [dma((2 * N_X - 1,))] * 2
     scratch += [dma((n_z - 1,))] * 2
@@ -555,7 +666,7 @@
             jax.ShapeDtypeStruct((1, ROWS), F32),
             jax.ShapeDtypeStruct((1, BLOCK), F32),
         ),
-        in_specs=[smem] * 3 + [vmem] * 10 + [hbm] * 9,
+        in_specs=[vmem] * 3 + [hbm] * 19,
         out_specs=(vmem, vmem),
         scratch_shapes=scratch,
         compiler_params=pltpu.CompilerParams(
@@ -563,13 +674,13 @@
         ),
         name="layer",
     )(
-        pred_device,
-        doc_ids,
-        valid_rows,
+        pred_device.reshape(1, 1),
+        doc_ids.reshape(1, 1),
+        valid_rows.reshape(1, 1),
         content_bias,
         position_bias,
         jnp.asarray(angle_basis()),
-        targets.reshape(ROWS, 1),
+        targets.reshape(1, ROWS),
         attn_gain.reshape(1, WIDTH),
         attn_shift.reshape(1, WIDTH),
         up_bias.reshape(1, WIDTH),
@@ -587,7 +698,17 @@
         w_vocab,
     )
     doc_slots = n_seg // 4
-    return token_terms.reshape(ROWS), docs[0, :doc_slots]
+    token_terms, docs = pl.pallas_call(
+        hand_over,
+        out_shape=(
+            jax.ShapeDtypeStruct((1, ROWS), F32),
+            jax.ShapeDtypeStruct((1, doc_slots), F32),
+        ),
+        in_specs=[vmem, vmem],
+        out_specs=(vmem, vmem),
+        name="results",
+    )(token_terms, docs)
+    return token_terms.reshape(ROWS), docs.reshape(doc_slots)
 
 
 def solution(mesh):

time: 90.2 us -> 89.1 us (0.988)
  local copies, waits for them, and re-layouts: 3.86 us -> 0 us
  Pallas kernels: 83.6 us -> 86.4 us
    pallas_call x1, Pallas kernels: 83.6 us -> 85.1 us  [on_device(): pl.pallas_call(functools.partial(kernel, n_seg), out_shape=(jax.ShapeDtyp...]
    reshape x1 -> x0, local copies, waits for them, and re-layouts: 1.53 us -> none  [on_device(): targets.reshape(ROWS, 1)]
    unnamed x1 -> x0, local copies, waits for them, and re-layouts: 1.25 us -> none
    pallas_call x0 -> x1, Pallas kernels: none -> 1.24 us  [on_device(): pl.pallas_call(hand_over, out_shape=(jax.ShapeDtypeStruct((1, ROWS), F32)...]
    squeeze x1 -> x0, local copies, waits for them, and re-layouts: 1.08 us -> none  [on_device(): return (token_terms.reshape(ROWS), docs[0, :doc_slots])]
where the time goes in v1:
time: 89.1 us; the launch traced here: 89 us
  Pallas kernels  86.4 us (97%)
  between operations  2.58 us (3%)
    pallas_call x1, Pallas kernels, on_device(): pl.pallas_call(functools.partial(kernel, n_seg), out_shape=(jax.ShapeDtyp...  85.1 us

profile of v1, /device:TPU:4, one launch (start us, length us, event | category | flops | bytes accessed | tf_op | source)
XLA Modules:
  0.0 89.0 jit_solution(4179587892855363188)
XLA Ops:
  2.6 85.1 %layer.1 = (f32[1,512]{1,0:T(1,128)}, f32[1,128]{1,0:T(1,128)}) custom-call(s32[1,1]{1,0:T(1,128)} %bitcast.12.pred_v, s32[1,1]{1,0:T(1,128)} %bitcast.13.doc_v, s32[1,1]{1,0:T(1,128)} %bitcast.14.valid_v, f32[4,64]{1,0:T(4,128)} %content_bias_h.1, f32[4,64]{1,0:T(4,128)} %position_bias_h.1, f32[4,32,512]{2,1,0:T(8,128)} %constant.2.clone.basis_h, ...), custom_call_target="tpu_custom_call" | custom-call | tf_op jit(solution)/shard_map/layer/pallas_call | solution.py:663
  87.7 1.2 %results.1 = (f32[1,512]{1,0:T(1,128)}, f32[1,16]{1,0:T(1,128)}) custom-call(f32[1,512]{1,0:T(1,128)} %get-tuple-element.6.token_i, f32[1,128]{1,0:T(1,128)} %get-tuple-element.7.doc_i), custom_call_target="tpu_custom_call" | custom-call | tf_op jit(solution)/shard_map/results/pallas_call | solution.py:701

commit v2 on v1

--- a/solution.py
+++ b/solution.py
@@ -18,7 +18,7 @@
 WIDTH = 1024
 BLOCK = 128
 HALF = 256
-PIECE = 64
+PIECE = 32
 FINE = 32
 MASKED = -1e30
 
@@ -93,6 +93,7 @@
     kv_x,
     kv_past,
     pos_past,
+    weights,
     top_own,
     sum_own,
     out_own,
@@ -101,7 +102,6 @@
     units,
     rs_send,
     rs_recv,
-    rs_pass,
     second,
     target_col,
     stats,
@@ -338,7 +338,8 @@
     use_cross = behind == 1 + 2 * core
     use_partner = behind == 2 * core - 1
     use_x = behind == 3 - 4 * core
-    for t in range(4):
+
+    def choose(t):
         remote(kv_own.at[t], kv_partner.at[t], partner_s.at[t], partner_r.at[t], partner).wait_recv()
         remote(kv_same.at[t], kv_cross.at[t], cross_s.at[t], cross_r.at[t], partner).wait_recv()
         remote(kv_same.at[t], kv_x.at[t], x_s.at[t], x_r.at[t], x_to).wait_recv()
@@ -346,157 +347,121 @@
         chosen = jnp.where(use_partner, kv_partner[t], chosen)
         kv_past[t] = jnp.where(use_x, kv_x[t], chosen)
 
-    side = (mp_at(1), mp_at(N_MP - 1))
-    source = (lax.rem(mp + N_MP - 1, N_MP), lax.rem(mp + 1, N_MP))
-    across = lax.rem(mp + 2, N_MP)
-
-    def pass_attended(b):
-        for k in range(2):
-            here = attended.at[source[k], b * BLOCK : (b + 1) * BLOCK]
-            remote(here, here, att_s.at[k, b], att_r.at[k, b], side[k]).wait_recv()
-            here = attended.at[source[k], b * BLOCK + k * PIECE : b * BLOCK + (k + 1) * PIECE]
-            send(here, here, att_s.at[2 + k, b], att_r.at[2 + k, b], side[k])
-
-    def attended_arrived(b):
-        for k in range(2):
-            here = attended.at[across, b * BLOCK + k * PIECE : b * BLOCK + (k + 1) * PIECE]
-            remote(here, here, att_s.at[2 + k, b], att_r.at[2 + k, b], side[k]).wait_recv()
-
-    for b in range(ROWS // BLOCK):
+    def origin(k):
+        return lax.rem(mp + N_MP - k, N_MP)
+
+    def attended_copy(b, k, owner):
+        here = attended.at[owner, b * BLOCK : (b + 1) * BLOCK]
+        return remote(here, here, att_s.at[k - 1, b], att_r.at[k - 1, b], mp_at(k))
+
+    def reduce_copy(b, k):
+        src = rs_send.at[b, lax.rem(mp + k, N_MP)]
+        return remote(src, rs_recv.at[b, k - 1], rs_s.at[k - 1, b], rs_r.at[k - 1, b], mp_at(k))
+
+    def second_copy(b, k, owner):
+        here = second.at[b, owner]
+        return remote(here, here, ag_s.at[k - 1, b], ag_r.at[k - 1, b], mp_at(k))
+
+    def begin(copy):
+        copy.start()
+        pending.append(copy)
+
+    def weigh(b):
         rows = slice(b * BLOCK, (b + 1) * BLOCK)
-
-        outcome = None
         for h in range(HEADS):
-            mine = of_head(h)
-            query = one_head(qc, rows, mine)
+            query = one_head(qc, rows, of_head(h))
             score = jnp.concatenate([dot_t(query, kv_past[c]) for c in range(2)], axis=1)
             score = jnp.where(has_memory, score + pos_past[h, rows, :], MASKED)
             before = top_own[h, rows, :]
             top = jnp.maximum(before, jnp.max(score, axis=-1, keepdims=True))
             weight = jnp.exp(score - top)
             fade = jnp.exp(before - top)
-            total = sum_own[h, rows, :] * fade + jnp.sum(weight, axis=-1, keepdims=True)
-            weight = weight.astype(BF16)
-            past = dot(weight[:, :HALF], kv_past[2]) + dot(weight[:, HALF:], kv_past[3])
-            done = (out_own[rows, :] * fade + past) / total
-            outcome = done if outcome is None else jnp.where(mine, done, outcome)
+            sum_own[h, rows, :] = sum_own[h, rows, :] * fade + jnp.sum(weight, axis=-1, keepdims=True)
+            top_own[h, rows, :] = fade
+            weights[h, rows, :] = weight.astype(BF16)
+
+    def attend(b):
+        rows = slice(b * BLOCK, (b + 1) * BLOCK)
+        outcome = None
+        for h in range(HEADS):
+            past = dot(weights[h, rows, :HALF], kv_past[2]) + dot(weights[h, rows, HALF:], kv_past[3])
+            done = (out_own[rows, :] * top_own[h, rows, :] + past) / sum_own[h, rows, :]
+            outcome = done if outcome is None else jnp.where(of_head(h), done, outcome)
         attended[mp, rows, :] = outcome.astype(BF16)
-        here = attended.at[mp, rows]
-        for k in range(2):
-            send(here, here, att_s.at[k, b], att_r.at[k, b], side[k])
-        if b > 0:
-            pass_attended(b - 1)
-
+        for k in (2, 1, 3):
+            begin(attended_copy(b, k, mp))
+
+    def feed(b):
+        rows = slice(b * BLOCK, (b + 1) * BLOCK)
+        for k in range(1, N_MP):
+            attended_copy(b, k, origin(k)).wait_recv()
+        head_sum = None
+        for g in range(N_MP):
+            term = dot(attended[g, rows, :], attn_out[g]).astype(BF16).astype(F32)
+            head_sum = term if head_sum is None else head_sum + term
+        total = emb[rows, :].astype(F32) + head_sum
+        first = normalize(total, attn_gain[...], attn_shift[...]).astype(BF16)
+        first_out[rows, :] = first
+        units[...] = jnp.maximum(dot(first, wup[...]) + up_bias[...], 0.0).astype(BF16)
+        terms = dot(units[...], wdown[...]).astype(BF16)
+        for d in range(N_MP):
+            rs_send[b, d] = terms[d * PIECE : (d + 1) * PIECE, :]
+        for k in (2, 1, 3):
+            begin(reduce_copy(b, k))
+
+    def finish_reduce(b):
+        total = rs_send[b, mp].astype(F32)
+        for k in range(1, N_MP):
+            reduce_copy(b, k).wait_recv()
+            total = total + rs_recv[b, k - 1].astype(F32)
+        at = pl.ds(pl.multiple_of(b * BLOCK + mp * PIECE, PIECE), PIECE)
+        total = first_out[at, :].astype(F32) + total + down_bias[...]
+        second[b, mp] = normalize(total, ffn_gain[...], ffn_shift[...]).astype(BF16)
+        for k in (2, 1, 3):
+            begin(second_copy(b, k, mp))
+
+    def second_arrived(b):
+        for k in range(1, N_MP):
+            second_copy(b, k, origin(k)).wait_recv()
+
+    choose(0)
+    choose(1)
+    weigh(0)
+    weigh(1)
+    choose(2)
+    choose(3)
+    attend(0)
+    attend(1)
+    weigh(2)
+    attend(2)
     for k in range(1, N_MP):
         there = lax.rem(mp + N_MP - k, N_MP)
         other = pl.ds(pl.multiple_of((1 - core) * BLOCK, BLOCK), BLOCK)
         here = attn_out.at[there, other]
         remote(here, here, aof_s.at[k - 1], aof_r.at[k - 1], partner).wait_recv()
-    loads[6].wait()
-    loads[7].wait()
-    loads[8].wait()
-
-    part_rows = (slice(0, PIECE // 2), slice(PIECE // 2, PIECE))
-
-    def reduce_copy(half, n):
-        k = n % 2
-        if n < 2:
-            src = rs_send.at[half, source[1 - k], part_rows[1 - k]]
-        elif n < 4:
-            src = rs_pass.at[half, k]
-        else:
-            src = rs_send.at[half, across, part_rows[k]]
-        return remote(src, rs_recv.at[half, n], rs_s.at[n, half], rs_r.at[n, half], side[k])
-
-    def start_reduce(half, n):
-        copy = reduce_copy(half, n)
-        copy.start()
-        pending.append(copy)
-
-    def pass_reduce(half):
-        for k in range(2):
-            reduce_copy(half, 4 + k).wait_recv()
-            mine = rs_send[half, source[1 - k], part_rows[k]].astype(F32)
-            rs_pass[half, k] = (mine + rs_recv[half, 4 + k].astype(F32)).astype(BF16)
-            start_reduce(half, 2 + k)
-
-    for half in range(2):
-        rows = slice(half * HALF, (half + 1) * HALF)
-        if half == 1:
-            attended_arrived(2)
-            attended_arrived(3)
-        else:
-            attended_arrived(0)
-            attended_arrived(1)
-        total = emb[rows, :].astype(F32)
-        head_sum = None
-        for g in range(N_MP):
-            term = dot(attended[g, rows, :], attn_out[g]).astype(BF16).astype(F32)
-            head_sum = term if head_sum is None else head_sum + term
-        first = normalize(total + head_sum, attn_gain[...], attn_shift[...]).astype(BF16)
-        first_out[rows, :] = first
-        if half == 0:
-            pass_attended(3)
-        units[...] = jnp.maximum(dot(first, wup[...]) + up_bias[...], 0.0).astype(BF16)
-        if half == 1:
-            pass_reduce(0)
-        terms = dot(units[...], wdown[...]).astype(BF16)
-        for d in range(N_MP):
-            rs_send[half, d] = terms[d * PIECE : (d + 1) * PIECE, :]
-        for n in (4, 5, 0, 1):
-            start_reduce(half, n)
-
-    def second_copy(half, n):
-        k = n % 2
-        if n < 2:
-            here = second.at[half, mp]
-        else:
-            here = second.at[half, source[k], part_rows[k]]
-        return remote(here, here, ag_s.at[n, half], ag_r.at[n, half], side[k])
-
-    def start_second(half, n):
-        copy = second_copy(half, n)
-        copy.start()
-        pending.append(copy)
-
-    def pass_second(half):
-        for k in range(2):
-            here = second.at[half, source[k]]
-            remote(here, here, ag_s.at[k, half], ag_r.at[k, half], side[k]).wait_recv()
-            start_second(half, 2 + k)
-
-    def second_arrived(half):
-        for k in range(2):
-            here = second.at[half, across, part_rows[k]]
-            remote(here, here, ag_s.at[2 + k, half], ag_r.at[2 + k, half], side[k]).wait_recv()
-
-    def finish_reduce(half):
-        for n in range(4):
-            reduce_copy(half, n).wait_recv()
-        for k in range(2):
-            total = rs_send[half, mp, part_rows[k]].astype(F32)
-            total = total + rs_recv[half, 1 - k].astype(F32) + rs_recv[half, 2 + k].astype(F32)
-            start = half * HALF + mp * PIECE + k * (PIECE // 2)
-            at = pl.ds(pl.multiple_of(start, PIECE // 2), PIECE // 2)
-            total = first_out[at, :].astype(F32) + total + down_bias[...]
-            total = normalize(total, ffn_gain[...], ffn_shift[...]).astype(BF16)
-            second[half, mp, part_rows[k]] = total
-        for n in range(2):
-            start_second(half, n)
-
+    for n in (6, 7, 8):
+        loads[n].wait()
+    weigh(3)
+    feed(0)
+    attend(3)
+    feed(1)
+    feed(2)
     finish_reduce(0)
-    pass_reduce(1)
-    pass_second(0)
+    feed(3)
     finish_reduce(1)
+    finish_reduce(2)
 
     tile = 512
     n_words = wvocab_h.shape[1]
-    for half in range(2):
-        rows = slice(half * HALF, (half + 1) * HALF)
-        second_arrived(half)
-        states = jnp.concatenate([second[half, d] for d in range(N_MP)], axis=0)
+    for blocks in ((0, 1), (2,), (3,)):
+        count = len(blocks) * BLOCK
+        rows = slice(blocks[0] * BLOCK, blocks[0] * BLOCK + count)
+        for b in blocks:
+            second_arrived(b)
+        states = [second[b, d] for b in blocks for d in range(N_MP)]
+        states = jnp.concatenate(states, axis=0)
         wanted = target_col[rows, 0:1].astype(jnp.int32) - mp * n_words
-        words = lax.broadcasted_iota(jnp.int32, (HALF, tile), 1)
+        words = lax.broadcasted_iota(jnp.int32, (count, tile), 1)
 
         def vocab_tile(n, carry, states=states, wanted=wanted, words=words):
             top, total, picked = carry
@@ -508,13 +473,13 @@
             hit = jnp.where(words == wanted - at, logits, 0.0)
             return new_top, total, picked + jnp.sum(hit, axis=1, keepdims=True)
 
-        zero = jnp.zeros((HALF, 1), F32)
-        found = (jnp.full((HALF, 1), -jnp.inf, F32), zero, zero)
+        zero = jnp.zeros((count, 1), F32)
+        found = (jnp.full((count, 1), -jnp.inf, F32), zero, zero)
         found = lax.fori_loop(0, 2, vocab_tile, found)
-        if half == 0:
-            pass_second(1)
+        if blocks[0] == 0:
+            finish_reduce(3)
         top, total, picked = lax.fori_loop(2, n_words // tile, vocab_tile, found)
-        lane = lax.broadcasted_iota(jnp.int32, (HALF, BLOCK), 1)
+        lane = lax.broadcasted_iota(jnp.int32, (count, BLOCK), 1)
         packed = jnp.where(lane == 0, top, jnp.where(lane == 1, total, picked))
         stats[mp, :, rows] = jnp.transpose(packed)[:8, :]
 
@@ -547,17 +512,19 @@
     for k in range(1, group):
         remote(doc_a.at[0], doc_a.at[k], da_s.at[k - 1], da_r.at[k - 1], group_at(k)).wait_recv()
     doc_b[0] = jnp.sum(doc_a[...], axis=0)
+    earlier = list(pending)
     for k in range(1, n_z):
         send(doc_b.at[0], doc_b.at[k], db_s.at[k - 1], db_r.at[k - 1], z_at(k))
+    for copy in earlier:
+        copy.wait_send()
+    for t in range(4):
+        remote(kv_own.at[t], kv_x.at[t], x_s.at[t], x_r.at[t], x_to).wait_send()
     for k in range(1, n_z):
         remote(doc_b.at[0], doc_b.at[k], db_s.at[k - 1], db_r.at[k - 1], z_at(k)).wait_recv()
     docs = jnp.sum(doc_b[...], axis=0)
     doc_o[...] = docs[0:1, :] / docs[1:2, :]
-
-    for copy in pending:
+    for copy in pending[len(earlier) :]:
         copy.wait_send()
-    for t in range(4):
-        remote(kv_own.at[t], kv_x.at[t], x_s.at[t], x_r.at[t], x_to).wait_send()
 
 
 def hand_over(token_i, doc_i, token_o, doc_o):
@@ -636,16 +603,16 @@
         kv,
         kv,
         pltpu.VMEM((HEADS, ROWS, ROWS), F32),
+        pltpu.VMEM((HEADS, ROWS, ROWS), BF16),
         column,
         column,
         pltpu.VMEM((ROWS, HALF), F32),
         pltpu.VMEM((N_MP, ROWS, HALF), BF16),
         pltpu.VMEM((ROWS, WIDTH), BF16),
-        pltpu.VMEM((HALF, WIDTH), BF16),
-        pltpu.VMEM((2, N_MP, PIECE, WIDTH), BF16),
-        pltpu.VMEM((2, 6, PIECE // 2, WIDTH), BF16),
-        pltpu.VMEM((2, 2, PIECE // 2, WIDTH), BF16),
-        pltpu.VMEM((2, N_MP, PIECE, WIDTH), BF16),
+        pltpu.VMEM((BLOCK, WIDTH), BF16),
+        pltpu.VMEM((4, N_MP, PIECE, WIDTH), BF16),
+        pltpu.VMEM((4, N_MP - 1, PIECE, WIDTH), BF16),
+        pltpu.VMEM((4, N_MP, PIECE, WIDTH), BF16),
         pltpu.VMEM((ROWS, 8), F32),
         pltpu.VMEM((N_MP, 8, ROWS), F32),
         pltpu.VMEM((2 * N_X, 8, BLOCK), F32),
@@ -654,17 +621,15 @@
     ]
     scratch += [dma((4,))] * 8
     scratch += [dma((N_MP - 1,))] * 4
-    scratch += [dma((4, 4))] * 2
-    scratch += [dma((6, 2))] * 2
-    scratch += [dma((4, 2))] * 2
+    scratch += [dma((N_MP - 1, 4))] * 6
     scratch += [dma((N_MP - 1,))] * 2
     scratch += [dma((2 * N_X - 1,))] * 2
     scratch += [dma((n_z - 1,))] * 2
     token_terms, docs = pl.pallas_call(
         functools.partial(kernel, n_seg),
         out_shape=(
-            jax.ShapeDtypeStruct((1, ROWS), F32),
-            jax.ShapeDtypeStruct((1, BLOCK), F32),
+            pltpu.VMEM((1, ROWS), F32),
+            pltpu.VMEM((1, BLOCK), F32),
         ),
         in_specs=[vmem] * 3 + [hbm] * 19,
         out_specs=(vmem, vmem),
@@ -707,7 +672,10 @@
         in_specs=[vmem, vmem],
         out_specs=(vmem, vmem),
         name="results",
-    )(token_terms, docs)
+    )(
+        pltpu.with_memory_space_constraint(token_terms, pltpu.VMEM),
+        pltpu.with_memory_space_constraint(docs, pltpu.VMEM),
+    )
     return token_terms.reshape(ROWS), docs.reshape(doc_slots)
 
 

time: 89.1 us -> 84.6 us (0.949)
  Pallas kernels: 86.4 us -> 82 us
    pallas_call x1, Pallas kernels: 85.1 us -> 81.4 us  [on_device(): pl.pallas_call(functools.partial(kernel, n_seg), out_shape=(pltpu.VMEM((1...]
where the time goes in v2:
time: 84.6 us; the launch traced here: 84.5 us
  Pallas kernels  82 us (97%)
  between operations  2.58 us (3%)
    pallas_call x1, Pallas kernels, on_device(): pl.pallas_call(functools.partial(kernel, n_seg), out_shape=(pltpu.VMEM((1...  81.4 us

profile of v2, /device:TPU:4, one launch (start us, length us, event | category | flops | bytes accessed | tf_op | source)
XLA Modules:
  0.0 84.5 jit_solution(16552589508585179527)
XLA Ops:
  2.6 81.4 %layer.1 = (f32[1,512]{1,0:T(1,128)S(1)}, f32[1,128]{1,0:T(1,128)S(1)}) custom-call(s32[1,1]{1,0:T(1,128)} %bitcast.12.pred_v, s32[1,1]{1,0:T(1,128)} %bitcast.13.doc_v, s32[1,1]{1,0:T(1,128)} %bitcast.14.valid_v, f32[4,64]{1,0:T(4,128)} %content_bias_h.1, f32[4,64]{1,0:T(4,128)} %position_bias_h.1, f32[4,32,512]{2,1,0:T(8,128)} %constant.2.clone.basis_h, ...), custom_call_target="tpu_custom_call" | custom-call | tf_op jit(solution)/shard_map/layer/pallas_call | solution.py:628
  84.0 0.6 results.1

commit v3 on v2

--- a/solution.py
+++ b/solution.py
@@ -442,8 +442,8 @@
     for n in (6, 7, 8):
         loads[n].wait()
     weigh(3)
+    attend(3)
     feed(0)
-    attend(3)
     feed(1)
     feed(2)
     finish_reduce(0)

time: 84.6 us -> 84.6 us (level)
  no operation moved by 1% of the time
where the time goes in v3:
time: 84.6 us; the launch traced here: 84.5 us
  Pallas kernels  81.9 us (97%)
  between operations  2.58 us (3%)
    pallas_call x1, Pallas kernels, on_device(): pl.pallas_call(functools.partial(kernel, n_seg), out_shape=(pltpu.VMEM((1...  81.3 us

profile of v3, /device:TPU:4, one launch (start us, length us, event | category | flops | bytes accessed | tf_op | source)
XLA Modules:
  0.0 84.5 jit_solution(17379084190577978092)
XLA Ops:
  2.6 81.3 %layer.1 = (f32[1,512]{1,0:T(1,128)S(1)}, f32[1,128]{1,0:T(1,128)S(1)}) custom-call(s32[1,1]{1,0:T(1,128)} %bitcast.12.pred_v, s32[1,1]{1,0:T(1,128)} %bitcast.13.doc_v, s32[1,1]{1,0:T(1,128)} %bitcast.14.valid_v, f32[4,64]{1,0:T(4,128)} %content_bias_h.1, f32[4,64]{1,0:T(4,128)} %position_bias_h.1, f32[4,32,512]{2,1,0:T(8,128)} %constant.2.clone.basis_h, ...), custom_call_target="tpu_custom_call" | custom-call | tf_op jit(solution)/shard_map/layer/pallas_call | solution.py:628
  83.9 0.6 results.1
